TPU v7x, 32 devices: a whole 2x2x4 slice. The times are simulated.
32 devices in a mesh: fz: 8 (over y, x, core), fxy: 4 (over z).
Axes of the slice: x: 2, y: 2, z: 4, core: 2. Of those that a mesh axis runs over, the one named last changes fastest.
Arguments:
- e_field: float32 [3, 64, 64, 512], P(None, 'fz', 'fxy'), may hold values from -6 to 6
- h_field: float32 [3, 64, 64, 512], P(None, 'fz', 'fxy'), may hold values from -6 to 6
- e_decay: float32 [64, 64, 512], P('fz', 'fxy'), may hold values from 0.6 to 1
- e_gain: float32 [64, 64, 512], P('fz', 'fxy'), may hold values from 0.2 to 0.6
- port_cell: int32 [8, 256], P('fz', 'fxy'), may hold values from 0 to 65535
- port_node: int32 [8, 256], P('fz', 'fxy'), may hold values from 0 to 2047
- port_conductance: float32 [8, 256], P('fz', 'fxy'), may hold values from 0.5 to 2
- inverse: float32 [8, 2048, 2048], P('fz', 'fxy'), may hold values from -1 to 2, as said below
- line_near: int32 [8, 128], P('fz'), may hold values from 0 to 2047
- line_far: int32 [8, 128], P('fz'), may hold values from 0 to 2047
- line_delay: int32 [8, 128], P('fz'), may hold values from 1 to 6
- line_imped: float32 [8, 128], P('fz'), may hold values from 0.5 to 4
- hist_near: float32 [8, 6, 128], P('fz'), may hold values from -6 to 6
- hist_far: float32 [8, 6, 128], P('fz'), may hold values from -6 to 6
Outputs:
- e_out: float32 [3, 64, 64, 512], P(None, 'fz', 'fxy')
- h_out: float32 [3, 64, 64, 512], P(None, 'fz', 'fxy')
- node_volt: float32 [8, 2048], P('fz', 'fxy')
- line_wave: float32 [8, 2, 128], P('fz')
Inputs may be any that keep to these rules, and one draw needn't show every extreme that they name: inverse[s] is symmetric for every s.
All inputs are finite; a program needn't handle non-finite values.
Results may differ from a plain program's by a relative error of at most 0.00029.
Values sent between devices are 32-bit elements; how exact they have to be, the bound alone decides.
A program may use at most 64 MiB of HBM per device.

v0:
```python
import functools

import jax
import jax.numpy as jnp
from jax import lax
from jax.experimental import pallas as pl
from jax.experimental.pallas import tpu as pltpu
from jax.sharding import PartitionSpec as P

STEPS = 4
LANES = 128
F32 = jnp.float32
BF16 = jnp.bfloat16
MESH = pl.DeviceIdType.MESH


def split3(x):
    a = x.astype(BF16)
    r = x - a.astype(F32)
    b = r.astype(BF16)
    c = (r - b.astype(F32)).astype(BF16)
    return a, b, c


def dot3(x, onehot, transposed):
    rows = x.shape[0]
    dims = (((1,), (1 if transposed else 0,)), ((), ()))
    if rows % 16 == 0:
        y = lax.dot_general(
            jnp.concatenate(split3(x), 0), onehot, dims, preferred_element_type=F32
        )
        return y[:rows] + y[rows : 2 * rows] + y[2 * rows :]
    a, b, c = (
        lax.dot_general(t, onehot, dims, preferred_element_type=F32) for t in split3(x)
    )
    return a + b + c


def kernel(
    e_in, h_in, decay_in, gain_in, port_cell_in, port_node_in, port_cond_in, inv_in,
    line_near_in, line_far_in, line_delay_in, line_imped_in, hist_near_in, hist_far_in,
    e_out, h_out, volt_out, wave_out,
    port_cell, port_node, port_cond, line_near, line_far, line_delay, line_imped,
    hist_near, hist_far,
    e, h, hz, ez_up, decay, gain, inv, cell_row, cell_y, node_hi, node_lo, pads,
    hx_send, hx, ex_send, ex, part_send, part, far_send, far, volt_send, volt,
    up_send, above, acc,
    load_sem, out_sem, face_send, face_recv, part_ss, part_rs, volt_ss, volt_rs,
):
    s, j = lax.axis_index("fz"), lax.axis_index("fxy")
    ns, nj = lax.axis_size("fz"), lax.axis_size("fxy")
    above_id, below_id = lax.rem(s + 1, ns), lax.rem(s + ns - 1, ns)
    right_id, left_id = lax.rem(j + 1, nj), lax.rem(j + nj - 1, nj)
    _, cz, cx, ny = e_in.shape
    cells = cz * cx
    block, nodes = inv_in.shape[1:]
    ports = port_cell_in.shape[1]
    lines = line_near_in.shape[1]
    depth = hist_near_in.shape[0]

    loads = [
        pltpu.make_async_copy(e_in, e.at[:, 0:cz], load_sem.at[0]),
        pltpu.make_async_copy(h_in, h.at[:, 1 : cz + 1], load_sem.at[1]),
        pltpu.make_async_copy(gain_in, gain, load_sem.at[2]),
        pltpu.make_async_copy(inv_in.at[0], inv, load_sem.at[3]),
        pltpu.make_async_copy(decay_in, decay, load_sem.at[4]),
    ]
    small = (
        (port_cell_in, port_cell), (port_node_in, port_node), (port_cond_in, port_cond),
        (line_near_in, line_near), (line_far_in, line_far), (line_delay_in, line_delay),
        (line_imped_in, line_imped), (hist_near_in, hist_near), (hist_far_in, hist_far),
    )
    small = [
        pltpu.make_async_copy(src, dst, load_sem.at[5 + k])
        for k, (src, dst) in enumerate(small)
    ]
    for copy in small + loads:
        copy.start()

    h[:, 0] = jnp.zeros((3, cx, ny), F32)
    e[:, cz] = jnp.zeros((3, cx, ny), F32)
    far[...] = jnp.zeros(far.shape, F32)
    above[...] = jnp.zeros(above.shape, F32)

    barrier = pltpu.get_barrier_semaphore()
    for other in (above_id, below_id):
        pl.semaphore_signal(barrier, inc=1, device_id={"fz": other}, device_id_type=MESH)
    for d in range(1, nj):
        pl.semaphore_signal(
            barrier, inc=1, device_id={"fxy": lax.rem(j + d, nj)}, device_id_type=MESH
        )

    for copy in small:
        copy.wait()

    pads[...] = jnp.full(pads.shape, -1, jnp.int32)
    pads[0:1, 0:ports] = port_cell[...]
    pads[1:2, 0:ports] = port_node[...]
    cell = pads[0:1, :]
    pnode = pads[1:2, :]
    valid = cell >= 0
    row = jnp.where(valid, cell // ny, -1)
    col = jnp.where(valid, cell % ny, -1)
    cell_row[...] = (lax.broadcasted_iota(jnp.int32, (cells, LANES), 0) == row).astype(F32)
    cell_y[...] = (
        (lax.broadcasted_iota(jnp.int32, (ny, LANES), 0) == col).astype(F32).astype(BF16)
    )
    for k, index in enumerate((pnode, line_near[...], line_far[...])):
        hi = jnp.where(index >= 0, index // block, -1)
        lo = jnp.where(index >= 0, index % block, -1)
        at = pl.ds(k * LANES, LANES)
        node_hi[:, at] = (
            lax.broadcasted_iota(jnp.int32, (node_hi.shape[0], LANES), 0) == hi
        ).astype(F32)
        node_lo[:, at] = (
            (lax.broadcasted_iota(jnp.int32, (block, LANES), 0) == lo)
            .astype(F32)
            .astype(BF16)
        )
    part_send[...] = jnp.zeros(part_send.shape, F32)
    part_send[0, 0:1, 0:ports] = port_cond[...]
    cond = part_send[0, 0:1, 0:LANES]

    has_above, has_below = s < ns - 1, s > 0
    has_right, has_left = j < nj - 1, j > 0

    def face(kind, step, src, dst, axis, other):
        return pltpu.make_async_remote_copy(
            src_ref=src, dst_ref=dst,
            send_sem=face_send.at[kind, step], recv_sem=face_recv.at[kind, step],
            device_id={axis: other}, device_id_type=MESH,
        )

    def up_copies(n):
        return (
            face(0, n, h.at[0:2, cz], hz.at[n], "fz", above_id),
            face(1, n, hx_send.at[n], hx.at[n], "fxy", right_id),
        )

    def down_copies(n):
        return (
            face(2, n, e.at[0:2, 0], ez_up.at[n], "fz", below_id),
            face(3, n, ex_send.at[n], ex.at[n], "fxy", left_id),
        )

    def far_copy(n):
        return face(4, n, far_send.at[n], far.at[n], "fz", above_id)

    def above_copy(n):
        return face(5, n, up_send.at[n], above.at[n], "fz", below_id)

    def start(cond_, copy):
        @pl.when(cond_)
        def _():
            copy.start()

    def wait_recv(cond_, copy):
        @pl.when(cond_)
        def _():
            copy.wait_recv()

    def wait_send(cond_, copy):
        @pl.when(cond_)
        def _():
            copy.wait_send()

    def gather_cells(plane):
        y = dot3(plane.reshape(cells, ny), cell_y[...], False)
        return jnp.sum(y * cell_row[...], axis=0, keepdims=True)

    def gather_nodes(volts, at):
        y = dot3(volts, node_lo[:, at], False)
        return jnp.sum(y * node_hi[0:nj, at], axis=0, keepdims=True)

    def scatter_nodes(values, at):
        rows = node_hi[:, at] * values
        return dot3(rows, node_lo[:, at], True)[0:nj]

    def gathers(n, send, recv, ss, rs):
        return [
            pltpu.make_async_remote_copy(
                src_ref=send.at[n], dst_ref=recv.at[n, j],
                send_sem=ss.at[n, d - 1], recv_sem=rs.at[n, d - 1],
                device_id={"fxy": lax.rem(j + d, nj)}, device_id_type=MESH,
            )
            for d in range(1, nj)
        ]

    at_port = pl.ds(0, LANES)
    at_near = pl.ds(LANES, LANES)
    at_far = pl.ds(2 * LANES, LANES)
    delay = line_delay[...]
    waves_a, waves_b = [], []

    def incoming(n, waves, hist):
        total = jnp.zeros((1, lines), F32)
        for k in range(1, depth + 1):
            value = waves[n - k] if n >= k else hist[k - n - 1]
            total = jnp.where(delay == k, value, total)
        return total

    def send_far(n, in_b):
        far_send[n] = scatter_nodes(-in_b, at_far)
        start(has_above, far_copy(n))

    def send_ports(n):
        ez = gather_cells(e[2, 0:cz])
        own = scatter_nodes(cond * ez, at_port)
        part_send[n] = own
        for copy in gathers(n, part_send, part, part_ss, part_rs):
            copy.start()
        return ez, own

    lane = lax.broadcasted_iota(jnp.int32, (cx, ny), 1)
    sub = lax.broadcasted_iota(jnp.int32, (cx, ny), 0)

    in_b = incoming(0, waves_a, hist_near)
    in_a = incoming(0, waves_b, hist_far)
    pl.semaphore_wait(barrier, nj + 1)
    send_far(0, in_b)
    loads[0].wait()
    ez, own = send_ports(0)
    loads[1].wait()
    for c in range(2):
        for z in range(cz):
            hx_send[0, c, z : z + 1, :] = h[1 + c, z + 1, cx - 1 : cx, :]
    copy_z, copy_x = up_copies(0)
    start(has_above, copy_z)
    start(has_right, copy_x)
    loads[2].wait()
    gain_port = gather_cells(gain[...])
    loads[3].wait()
    loads[4].wait()

    for n in range(STEPS):
        near_src = scatter_nodes(-in_a, at_near)
        wait_recv(has_below, far_copy(n))
        port_copies = gathers(n, part_send, part, part_ss, part_rs)
        for copy in port_copies:
            copy.wait_recv()
        part[n, j] = own
        totals = part[n, 0]
        for k in range(1, nj):
            totals = totals + part[n, k]
        totals = totals + (near_src + far[n])
        chunk = 32

        @pl.loop(0, block // chunk)
        def _(r):
            at = pl.ds(pl.multiple_of(r * chunk, chunk), chunk)
            value = jnp.zeros((chunk, LANES), F32)
            for k in range(nodes // LANES):
                q, w = divmod(k * LANES, block)
                value = value + inv[at, k * LANES : (k + 1) * LANES] * totals[
                    q : q + 1, w : w + LANES
                ]
            acc[at, :] = value

        terms = jnp.concatenate(split3(acc[...]), 1)
        local_volt = lax.dot_general(
            jnp.ones((16, 3 * LANES), BF16), terms, (((1,), (1,)), ((), ())),
            preferred_element_type=F32,
        )[0:1]
        volt_send[n] = local_volt
        volt_copies = gathers(n, volt_send, volt, volt_ss, volt_rs)
        for copy in volt_copies:
            copy.start()

        copy_z, copy_x = up_copies(n)

        @pl.loop(0, cz)
        def _(z):
            hx_, hy_, hz_ = (h[c, z + 1] for c in range(3))
            lx, ly = h[0, z], h[1, z]

            def by(f):
                return f - jnp.where(lane == 0, 0.0, pltpu.roll(f, 1, 1))

            def bx(f):
                return f - jnp.where(sub == 0, 0.0, pltpu.roll(f, 1, 0))

            g, q = gain[z], decay[z]
            e[0, z] = q * e[0, z] + g * (by(hz_) - (hy_ - ly))
            e[1, z] = q * e[1, z] + g * ((hx_ - lx) - bx(hz_))
            e[2, z] = q * e[2, z] + g * (bx(hy_) - by(hx_))

        down_z, down_x = down_copies(n)

        @pl.when(has_left)
        def _():
            copy_x.wait_recv()
            for z in range(cz):
                g = gain[z, 0:1, :]
                e[1, z, 0:1, :] = e[1, z, 0:1, :] + g * hx[n, 1, z : z + 1, :]
                e[2, z, 0:1, :] = e[2, z, 0:1, :] - g * hx[n, 0, z : z + 1, :]

        @pl.when(has_below)
        def _():
            copy_z.wait_recv()
            g = gain[0]
            e[0, 0] = e[0, 0] + g * hz[n, 1]
            e[1, 0] = e[1, 0] - g * hz[n, 0]
            down_z.start()

        for copy in volt_copies:
            copy.wait_recv()
        volt[n, j] = local_volt
        volts = jnp.concatenate([volt[n, k] for k in range(nj)], 0)
        up_send[n] = volts
        start(has_below, above_copy(n))
        drop = gain_port * (cond * (ez - gather_nodes(volts, at_port)))
        change = dot3(cell_row[...] * drop, cell_y[...], True)
        e[2, 0:cz] = e[2, 0:cz] - change.reshape(cz, cx, ny)
        for c in range(2):
            for z in range(cz):
                ex_send[n, c, z : z + 1, :] = e[1 + c, z, 0:1, :]
        start(has_left, down_x)

        out_a = -2.0 * gather_nodes(volts, at_near) / line_imped[...] - in_a
        waves_a.append(out_a)
        old_b, old_ez = in_b, ez
        if n + 1 < STEPS:
            ez, own = send_ports(n + 1)
            in_b = incoming(n + 1, waves_a, hist_near)
            send_far(n + 1, in_b)
        else:
            e_store = pltpu.make_async_copy(e.at[:, 0:cz], e_out, out_sem.at[0])
            e_store.start()

        wait_send(has_above, copy_z)
        wait_send(has_right, copy_x)

        @pl.loop(0, cz)
        def _(z):
            ex_, ey_, ez_ = (e[c, z] for c in range(3))
            ux, uy = e[0, z + 1], e[1, z + 1]

            def dy(f):
                return jnp.where(lane == ny - 1, 0.0, pltpu.roll(f, ny - 1, 1)) - f

            def dx(f):
                return jnp.where(sub == cx - 1, 0.0, pltpu.roll(f, cx - 1, 0)) - f

            h[0, z + 1] = h[0, z + 1] - 0.5 * (dy(ez_) - (uy - ey_))
            h[1, z + 1] = h[1, z + 1] - 0.5 * ((ux - ex_) - dx(ez_))
            h[2, z + 1] = h[2, z + 1] - 0.5 * (dx(ey_) - dy(ex_))

        @pl.when(has_above)
        def _():
            down_z.wait_recv()
            h[0, cz] = h[0, cz] + 0.5 * ez_up[n, 1]
            h[1, cz] = h[1, cz] - 0.5 * ez_up[n, 0]

        if n + 1 < STEPS:
            next_z, next_x = up_copies(n + 1)
        at_x = slice(cx - 1, cx)

        @pl.when(has_right)
        def _():
            down_x.wait_recv()
            for z in range(cz):
                new_y = h[1, z + 1, at_x, :] + 0.5 * ex[n, 1, z : z + 1, :]
                new_z = h[2, z + 1, at_x, :] - 0.5 * ex[n, 0, z : z + 1, :]
                h[1, z + 1, at_x, :] = new_y
                h[2, z + 1, at_x, :] = new_z
                if n + 1 < STEPS:
                    hx_send[n + 1, 0, z : z + 1, :] = new_y
                    hx_send[n + 1, 1, z : z + 1, :] = new_z
            if n + 1 < STEPS:
                next_x.start()

        if n + 1 < STEPS:
            start(has_above, next_z)
        else:
            h_store = pltpu.make_async_copy(h.at[:, 1 : cz + 1], h_out, out_sem.at[1])
            h_store.start()

        wait_recv(has_above, above_copy(n))
        out_b = -2.0 * gather_nodes(above[n], at_far) / line_imped[...] - old_b
        waves_b.append(out_b)
        if n + 1 < STEPS:
            in_a = incoming(n + 1, waves_b, hist_far)

        wait_send(has_below, down_z)
        wait_send(has_left, down_x)
        wait_send(has_above, far_copy(n))
        wait_send(has_below, above_copy(n))
        for copy in port_copies + volt_copies:
            copy.wait_send()

    volt_out[...] = local_volt
    wave_out[0, 0:1, :] = out_a
    wave_out[0, 1:2, :] = out_b
    e_store.wait()
    h_store.wait()


def local(*args):
    e_field, inverse = args[0], args[7]
    nj = lax.axis_size("fxy")
    _, cz, cx, ny = e_field.shape
    _, block, nodes = inverse.shape
    lines = args[8].shape[1]
    args = [*args[:12], *(a.transpose(1, 0, 2) for a in args[12:])]
    vmem, any_ = pl.BlockSpec(memory_space=pltpu.VMEM), pl.BlockSpec(memory_space=pl.ANY)
    small = [a for i, a in enumerate(args) if i not in (0, 1, 2, 3, 7)]
    hbm = pl.BlockSpec(memory_space=pltpu.HBM)
    rows = -(-nj // 16) * 16
    dma = pltpu.SemaphoreType.DMA
    v = pltpu.VMEM
    return pl.pallas_call(
        kernel,
        out_shape=(
            jax.ShapeDtypeStruct(e_field.shape, F32),
            jax.ShapeDtypeStruct(e_field.shape, F32),
            jax.ShapeDtypeStruct((1, block), F32),
            jax.ShapeDtypeStruct((1, 2, lines), F32),
        ),
        in_specs=[hbm] * len(args),
        out_specs=(any_, any_, vmem, vmem),
        scratch_shapes=[
            *[v(a.shape, a.dtype) for a in small],
            v((3, cz + 1, cx, ny), F32),
            v((3, cz + 1, cx, ny), F32),
            v((STEPS, 2, cx, ny), F32),
            v((STEPS, 2, cx, ny), F32),
            v((cz, cx, ny), F32),
            v((cz, cx, ny), F32),
            v((block, nodes), F32),
            v((cz * cx, LANES), F32),
            v((ny, LANES), BF16),
            v((rows, 3 * LANES), F32),
            v((block, 3 * LANES), BF16),
            v((8, LANES), jnp.int32),
            v((STEPS, 2, cz, ny), F32),
            v((STEPS, 2, cz, ny), F32),
            v((STEPS, 2, cz, ny), F32),
            v((STEPS, 2, cz, ny), F32),
            v((STEPS, nj, block), F32),
            v((STEPS, nj, nj, block), F32),
            v((STEPS, nj, block), F32),
            v((STEPS, nj, block), F32),
            v((STEPS, 1, block), F32),
            v((STEPS, nj, 1, block), F32),
            v((STEPS, nj, block), F32),
            v((STEPS, nj, block), F32),
            v((block, LANES), F32),
            dma((5 + len(small),)),
            dma((2,)),
            dma((6, STEPS)),
            dma((6, STEPS)),
            dma((STEPS, nj - 1)),
            dma((STEPS, nj - 1)),
            dma((STEPS, nj - 1)),
            dma((STEPS, nj - 1)),
        ],
        compiler_params=pltpu.CompilerParams(
            collective_id=0, has_side_effects=True, vmem_limit_bytes=67043328
        ),
    )(*args)


def solution(mesh):
    placed = (
        P(None, "fz", "fxy", None),
        P(None, "fz", "fxy", None),
        P("fz", "fxy", None),
        P("fz", "fxy", None),
        P("fz", "fxy"),
        P("fz", "fxy"),
        P("fz", "fxy"),
        P("fz", "fxy", None),
        P("fz", None),
        P("fz", None),
        P("fz", None),
        P("fz", None),
        P("fz", None, None),
        P("fz", None, None),
    )
    return jax.shard_map(
        local,
        mesh=mesh,
        in_specs=placed,
        out_specs=(
            P(None, "fz", "fxy", None),
            P(None, "fz", "fxy", None),
            P("fz", "fxy"),
            P("fz", None, None),
        ),
        check_vma=False,
    )
```

profile of v0, /device:TPU:0, one launch (start us, length us, event | category | flops | bytes accessed | tf_op | source)
XLA Modules:
  0.0 53.2 jit_solution(15893633973977465958)
XLA Ops:
  0.6 45.9 %shard_map.165 = (f32[3,8,16,512]{3,2,1,0:T(8,128)}, f32[3,8,16,512]{3,2,1,0:T(8,128)}, f32[1,512]{1,0:T(1,128)}, f32[1,2,128]{2,1,0:T(2,128)}) custom-call(f32[3,8,16,512]{3,2,1,0:T(8,128)} %e_in.1, f32[3,8,16,512]{3,2,1,0:T(8,128)} %h_in.1, f32[8,16,512]{2,1,0:T(8,128)} %decay_in.1, f32[8,16,512]{2,1,0:T(8,128)} %gain_in.1, s32[1,64]{1,0:T(1,128)} %port_cell_in.1, ...), custom_call_target="tpu_custom_call" | custom-call | tf_op jit(solution)/shard_map/pallas_call | solution.py:411
  46.5 2.1 %copy.22 = f32[3,8,16,512]{3,2,1,0:T(8,128)} copy(f32[3,8,16,512]{3,2,1,0:T(8,128)} %get-tuple-element.8) | data formatting | bytes 1572864
  48.6 2.1 %copy.23 = f32[3,8,16,512]{3,2,1,0:T(8,128)} copy(f32[3,8,16,512]{3,2,1,0:T(8,128)} %get-tuple-element.9) | data formatting | bytes 1572864
  50.7 1.2 %copy.24 = f32[1,512]{1,0:T(1,128)} copy(f32[1,512]{1,0:T(1,128)} %get-tuple-element.10) | data formatting | bytes 4096
  52.0 1.2 %copy.25 = f32[1,2,128]{2,1,0:T(2,128)} copy(f32[1,2,128]{2,1,0:T(2,128)} %get-tuple-element.11) | data formatting | bytes 2048
where the time goes:
time: 53.4 us; the launch traced here: 53.2 us
  Pallas kernels  45.9 us (86%)
  local copies, waits for them, and re-layouts  6.64 us (12%)
  between operations  0.65 us (1%)
    pallas_call x1, Pallas kernels, local(): pl.pallas_call(kernel, out_shape=(jax.ShapeDtypeStruct(e_field.shape, F32...  45.9 us
    unnamed x4, local copies, waits for them, and re-layouts  6.64 us

commit v1 on v0

v1 whole, which is shorter than its diff:
```python
import jax
import jax.numpy as jnp
from jax import lax
from jax.experimental import pallas as pl
from jax.experimental.pallas import tpu as pltpu
from jax.sharding import PartitionSpec as P

STEPS = 4
LANES = 128
F32 = jnp.float32
BF16 = jnp.bfloat16
I32 = jnp.int32
MESH = pl.DeviceIdType.MESH
ROWS = (((1,), (0,)), ((), ()))
COLS = (((1,), (1,)), ((), ()))


def iota(shape, dim):
    return lax.broadcasted_iota(I32, shape, dim)


def parts3(x):
    a = x.astype(BF16).astype(F32)
    r = x - a
    b = r.astype(BF16).astype(F32)
    return a, b, r - b


def dot(x, y, dims=ROWS):
    return lax.dot_general(x, y, dims, preferred_element_type=F32)


def dot3(x, onehot, dims):
    rows = x.shape[0]
    parts = list(parts3(x))
    pad = -3 * rows % 16
    if pad:
        parts.append(jnp.zeros((pad, x.shape[1]), F32))
    y = dot(jnp.concatenate(parts, 0).astype(BF16), onehot, dims)
    return y[:rows] + y[rows : 2 * rows] + y[2 * rows : 3 * rows]


def fold3(x):
    a, b, c = parts3(jnp.broadcast_to(x, (16, x.shape[1])))
    r = iota(a.shape, 0)
    x = jnp.where(r == 0, a, jnp.where(r == 1, b, jnp.where(r == 2, c, 0.0)))
    return x.astype(BF16)


def sum3(y):
    return y[0:1] + y[1:2] + y[2:3]


def column(row):
    return jnp.concatenate(
        [
            jnp.broadcast_to(row[:, t : t + LANES], (LANES, LANES)).T
            for t in range(0, row.shape[1], LANES)
        ],
        0,
    )


def kernel(
    e_in, h_in, decay_in, gain_in, port_cell_in, port_node_in, port_cond_in, inv_in,
    line_near_in, line_far_in, line_delay_in, line_imped_in, hist_near_in, hist_far_in,
    e, h, volt_out, wave_out,
    port_cell, port_node, port_cond, line_near, line_far, line_delay, line_imped,
    hist_near, hist_far,
    e_top, decay, gain, gain_top, gain_send, gain_right, inv, inv2, pick, picked, own_pick,
    same, left, mat, cell_row, cell_y, row_right, y_right, node_hi, node_lo, pads,
    info_send, info, line_send, line_info, pre_send, pre, y_send, y, below, above,
    hz, ez_up, hx_send, hx, ex_send, ex, corner_send, corner_a, corner_b, acc,
    load_sem, face_ss, face_rs, info_ss, info_rs, pre_ss, pre_rs, y_ss, y_rs,
    up_ss, up_rs, down_ss, down_rs,
):
    s, j = lax.axis_index("fz"), lax.axis_index("fxy")
    ns, nj = lax.axis_size("fz"), lax.axis_size("fxy")
    above_id, below_id = lax.rem(s + 1, ns), lax.rem(s + ns - 1, ns)
    right_id, left_id = lax.rem(j + 1, nj), lax.rem(j + nj - 1, nj)
    has_above, has_below = s < ns - 1, s > 0
    has_right, has_left = j < nj - 1, j > 0
    _, cz, cx, ny = e_in.shape
    cells = cz * cx
    block, nodes = inv_in.shape[1:]
    ports = port_cell_in.shape[1]
    lines = line_near_in.shape[1]
    depth = hist_near_in.shape[0]
    pack = LANES // ports
    tiles = nj // pack
    np_ = nj * ports
    nt = np_ + 2 * lines

    loads = [
        pltpu.make_async_copy(e_in, e, load_sem.at[0]),
        pltpu.make_async_copy(gain_in, gain, load_sem.at[1]),
        pltpu.make_async_copy(h_in, h, load_sem.at[2]),
        pltpu.make_async_copy(decay_in, decay, load_sem.at[3]),
        pltpu.make_async_copy(inv_in.at[0], inv, load_sem.at[4]),
    ]
    small = (
        (port_cell_in, port_cell), (port_node_in, port_node), (port_cond_in, port_cond),
        (line_near_in, line_near), (line_far_in, line_far), (line_delay_in, line_delay),
        (line_imped_in, line_imped), (hist_near_in, hist_near), (hist_far_in, hist_far),
    )
    small = [
        pltpu.make_async_copy(src, dst, load_sem.at[5 + k])
        for k, (src, dst) in enumerate(small)
    ]
    for copy in small + loads:
        copy.start()

    e_top[...] = jnp.zeros(e_top.shape, F32)
    below[...] = jnp.zeros(below.shape, F32)
    above[...] = jnp.zeros(above.shape, F32)
    corner_a[...] = jnp.zeros(corner_a.shape, F32)
    corner_b[...] = jnp.zeros(corner_b.shape, F32)
    line_info[...] = (iota(line_info.shape, 0) == 2).astype(F32)

    barrier = pltpu.get_barrier_semaphore()
    for other in (above_id, below_id):
        for d in range(nj):
            pl.semaphore_signal(
                barrier, inc=1, device_id={"fz": other, "fxy": lax.rem(j + d, nj)},
                device_id_type=MESH,
            )
    for d in range(1, nj):
        pl.semaphore_signal(
            barrier, inc=1, device_id={"fxy": lax.rem(j + d, nj)}, device_id_type=MESH
        )

    def remote(src, dst, ss, rs, **where):
        return pltpu.make_async_remote_copy(
            src_ref=src, dst_ref=dst, send_sem=ss, recv_sem=rs,
            device_id=where, device_id_type=MESH,
        )

    def face(kind, n, src, dst, **where):
        return remote(src, dst, face_ss.at[kind, n], face_rs.at[kind, n], **where)

    def when(cond, copies, act):
        @pl.when(cond)
        def _():
            for copy in copies:
                getattr(copy, act)()

    def up_z(n):
        return face(0, n, h.at[0:2, cz - 1], hz.at[n], fz=above_id)

    def up_x(n):
        return face(1, n, hx_send.at[n], hx.at[n], fxy=right_id)

    def down_z(n):
        return face(2, n, e.at[0:2, 0], ez_up.at[n], fz=below_id)

    def down_x(n):
        return face(3, n, ex_send.at[n], ex.at[n], fxy=left_id)

    def corner_down(n):
        return face(4, n, corner_send.at[n, 0], corner_a.at[n], fz=below_id, fxy=right_id)

    def corner_up(n):
        return face(5, n, corner_send.at[n, 1], corner_b.at[n], fz=above_id, fxy=left_id)

    line_copy = face(6, 0, line_send, line_info, fz=above_id)
    gain_z = face(6, 1, gain.at[0], gain_top, fz=below_id)
    gain_x = face(6, 2, gain_send, gain_right, fxy=left_id)

    def spread(src, dst, ss, rs):
        return [
            remote(src, dst, ss.at[d - 1], rs.at[d - 1], fxy=lax.rem(j + d, nj))
            for d in range(1, nj)
        ]

    def spread_z(src, dst, ss, rs, to):
        return [
            remote(src, dst, ss.at[d], rs.at[d], fz=to, fxy=lax.rem(j + d, nj))
            for d in range(nj)
        ]

    info_copies = spread(info_send, info.at[j], info_ss, info_rs)

    def pre_copies(n):
        return spread(pre_send.at[n], pre.at[n, j], pre_ss.at[n], pre_rs.at[n])

    def y_copies(n):
        return (
            spread(y_send.at[n], y.at[n, j], y_ss.at[n], y_rs.at[n]),
            spread_z(
                y_send.at[n, :, np_ : np_ + lines], below.at[n, j],
                up_ss.at[n], up_rs.at[n], above_id,
            ),
            spread_z(
                y_send.at[n, :, np_ + lines : nt], above.at[n, j],
                down_ss.at[n], down_rs.at[n], below_id,
            ),
        )

    def send_y(n, value):
        y_send[n] = value
        y[n, j] = value
        slab, up, down = y_copies(n)
        when(has_above, up, "start")
        when(has_below, down, "start")
        for copy in slab:
            copy.start()

    def send_h(n):
        for c in range(2):
            for z in range(cz):
                hx_send[n, c, z : z + 1, :] = h[1 + c, z, cx - 1 : cx, :]
        corner_send[n, 0] = h[2, 0, cx - 1 : cx, :]
        corner_send[n, 1] = h[0, cz - 1, 0:1, :]
        when(has_above, [up_z(n)], "start")
        when(has_right, [up_x(n)], "start")
        when(has_below & has_right, [corner_down(n)], "start")
        when(has_above & has_left, [corner_up(n)], "start")

    def send_e(n):
        for c in range(2):
            for z in range(cz):
                ex_send[n, c, z : z + 1, :] = e[1 + c, z, 0:1, :]
        when(has_below, [down_z(n)], "start")
        when(has_left, [down_x(n)], "start")

    lane = iota((cx, ny), 1)
    sub = iota((cx, ny), 0)

    def update_e():
        def plane(z, lower):
            hx_, hy_, hz_ = (h[c, z] for c in range(3))
            dx, dy = hx_, hy_
            if lower is not None:
                dx, dy = hx_ - h[0, lower], hy_ - h[1, lower]

            def by(f):
                return f - jnp.where(lane == 0, 0.0, pltpu.roll(f, 1, 1))

            def bx(f):
                return f - jnp.where(sub == 0, 0.0, pltpu.roll(f, 1, 0))

            g, q = gain[z], decay[z]
            e[0, z] = q * e[0, z] + g * (by(hz_) - dy)
            e[1, z] = q * e[1, z] + g * (dx - bx(hz_))
            e[2, z] = q * e[2, z] + g * (bx(hy_) - by(hx_))

        plane(0, None)

        @pl.loop(1, cz)
        def _(z):
            plane(z, z - 1)

    def update_h():
        def plane(z, ux, uy):
            ex_, ey_, ez_ = (e[c, z] for c in range(3))

            def dy(f):
                return jnp.where(lane == ny - 1, 0.0, pltpu.roll(f, ny - 1, 1)) - f

            def dx(f):
                return jnp.where(sub == cx - 1, 0.0, pltpu.roll(f, cx - 1, 0)) - f

            h[0, z] = h[0, z] - 0.5 * (dy(ez_) - (uy - ey_))
            h[1, z] = h[1, z] - 0.5 * ((ux - ex_) - dx(ez_))
            h[2, z] = h[2, z] - 0.5 * (dx(ey_) - dy(ex_))

        @pl.loop(0, cz - 1)
        def _(z):
            plane(z, e[0, z + 1], e[1, z + 1])

        plane(cz - 1, e_top[0], e_top[1])

    for copy in small:
        copy.wait()

    pads[...] = jnp.zeros(pads.shape, F32)
    pads[0:1, 0:ports] = (port_cell[...] + 1).astype(F32)
    pads[1:2, 0:ports] = (port_node[...] + 1).astype(F32)
    pads[2:3, 0:ports] = port_cond[...]
    rows = pltpu.roll(pads[...], ports * lax.rem(j, pack), 1)
    info_send[...] = rows
    cell = rows[0:1].astype(I32) - 1
    valid = cell >= 0
    cell_row[...] = (
        iota((cells, LANES), 0) == jnp.where(valid, cell // ny, -1)
    ).astype(F32)
    cell_y[...] = (
        (iota((ny, LANES), 0) == jnp.where(valid, cell % ny, -1)).astype(F32).astype(BF16)
    )
    line_send[...] = jnp.zeros(line_send.shape, F32)
    line_send[0:1, :] = (line_far[...] + 1).astype(F32)
    line_send[1:2, :] = line_delay[...].astype(F32)
    line_send[2:3, :] = line_imped[...]
    for k in range(depth):
        line_send[3 + k : 4 + k, :] = hist_near[k]
        line_send[3 + depth + k : 4 + depth + k, :] = hist_far[k]

    def gather_cells(f):
        value = dot3(f.reshape(cells, ny), cell_y[...], ROWS)
        return jnp.sum(value * cell_row[...], axis=0, keepdims=True)

    loads[0].wait()
    info_send[4:5, :] = gather_cells(e[2])
    loads[1].wait()
    info_send[3:4, :] = gather_cells(gain[...])
    for z in range(cz):
        gain_send[z : z + 1, :] = gain[z, 0:1, :]
    info[j] = info_send[...]

    pl.semaphore_wait(barrier, nj - 1 + 2 * nj)
    for copy in info_copies:
        copy.start()
    when(has_above, [line_copy], "start")
    loads[2].wait()
    send_h(0)
    loads[3].wait()
    update_e()
    send_e(0)
    when(has_below, [gain_z], "start")
    when(has_left, [gain_x], "start")
    loads[4].wait()

    chunk = 32

    @pl.loop(0, block // chunk)
    def _(r):
        at = pl.ds(pl.multiple_of(r * chunk, chunk), chunk)
        x = inv[at, :]
        high = x.astype(BF16)
        inv2[at, :] = high
        inv2[pl.ds(pl.multiple_of(block + r * chunk, chunk), chunk), :] = (
            x - high.astype(F32)
        ).astype(BF16)

    when(has_below, [line_copy], "wait_recv")
    for copy in info_copies:
        copy.wait_recv()

    everyone = jnp.concatenate(
        [sum(info[t * pack + k] for k in range(pack)) for t in range(tiles)], 1
    )
    cell_all = everyone[0:1] - 1.0
    cond_all, gain_all = everyone[2:3], everyone[3:4]
    near_far = [line_near[...], line_info[0:1, :].astype(I32) - 1]
    index = jnp.concatenate([everyone[1:2].astype(I32) - 1, *near_far], 1)
    high = jnp.where(index >= 0, index // block, -1)
    low = jnp.where(index >= 0, index % block, -1)
    node_hi[...] = (iota(node_hi.shape, 0) == high).astype(F32)
    node_lo[...] = (iota(node_lo.shape, 0) == low).astype(F32).astype(BF16)

    delay = jnp.concatenate([line_delay[...].astype(F32), line_info[1:2, :]], 0)
    scale = -2.0 / jnp.concatenate([line_imped[...], line_info[2:3, :]], 0)
    past_a = [
        jnp.concatenate([hist_near[k], line_info[3 + k : 4 + k, :]], 0)
        for k in range(depth)
    ]
    past_b = [
        jnp.concatenate([hist_far[k], line_info[3 + depth + k : 4 + depth + k, :]], 0)
        for k in range(depth)
    ]
    waves_a, waves_b = [], []

    def incoming(n, waves, past):
        total = jnp.zeros((2, lines), F32)
        for k in range(1, depth + 1):
            value = waves[n - k] if n >= k else past[k - n - 1]
            total = jnp.where(delay == k, value, total)
        return total

    def sources(n, ez):
        in_a, in_b = incoming(n, waves_b, past_b), incoming(n, waves_a, past_a)
        return in_a, in_b, jnp.concatenate([cond_all * ez, -in_a[0:1], -in_b[1:2]], 1)

    def own_volts(src):
        totals = dot3(node_hi[...] * src, node_lo[...], COLS)[0:nj]

        @pl.loop(0, block // chunk)
        def _(r):
            at = pl.ds(pl.multiple_of(r * chunk, chunk), chunk)
            value = jnp.zeros((chunk, LANES), F32)
            for k in range(nodes // LANES):
                q, w = divmod(k * LANES, block)
                value = value + inv[at, k * LANES : (k + 1) * LANES] * totals[
                    q : q + 1, w : w + LANES
                ]
            acc[at, :] = value

        terms = jnp.concatenate(parts3(acc[...]), 1).astype(BF16)
        return dot(jnp.ones((16, 3 * LANES), BF16), terms, COLS)[0:1]

    key = cell_all + ((iota((1, np_), 1) // ports) * (cells * ny)).astype(F32)
    key_col = column(key)
    for t in range(0, np_, LANES):
        at = slice(t, t + LANES)
        same[:, at] = (key_col == key[:, at]).astype(F32) * cond_all[:, at]

    ez = everyone[4:5]
    in_a, in_b, src = sources(0, ez)
    v0 = sum3(dot(fold3(own_volts(src)), node_lo[...]))
    v0 = jnp.where(high == j, v0, 0.0)
    drive = lax.dot_general(
        jnp.broadcast_to(v0[:, 0:np_], (8, np_)), same[...], COLS,
        precision=lax.Precision.HIGHEST, preferred_element_type=F32,
    )[0:1]
    send_y(0, jnp.concatenate([gain_all * drive, v0[:, np_:]], 1))

    neighbour = info[right_id]
    cell_r = neighbour[0:1].astype(I32) - 1
    gain_r = neighbour[3:4]
    valid_r = (cell_r >= 0) & (lax.rem(cell_r // ny, cx) == 0) & has_right
    row_right[...] = (
        iota((cz, LANES), 0) == jnp.where(valid_r, cell_r // (cx * ny), -1)
    ).astype(F32)
    y_right[...] = (
        (iota((ny, LANES), 0) == jnp.where(valid_r, cell_r % ny, -1))
        .astype(F32)
        .astype(BF16)
    )

    def send_pre(n):
        value = gather_cells(e[2])
        side = dot3(hx_send[n - 1, 0], y_right[...], ROWS) * row_right[...]
        side = -gain_r * jnp.sum(side, axis=0, keepdims=True)
        for t in range(tiles):
            at = slice(t * LANES, (t + 1) * LANES)
            both = jnp.where(j // pack == t, value, 0.0)
            both = both + jnp.where(right_id // pack == t, side, 0.0)
            pre_send[n, :, at] = both
        pre[n, j] = pre_send[n]
        for copy in pre_copies(n):
            copy.start()

    send_pre(1)

    cond_col = column(cond_all)
    gain_col = column(gain_all)
    load, first = [], []
    for t in range(0, np_, LANES):
        hit = key_col == key[:, t : t + LANES]
        load.append(jnp.sum(jnp.where(hit, cond_col, 0.0), axis=0, keepdims=True))
        earlier = hit & (iota(hit.shape, 0) < iota(hit.shape, 1) + t)
        first.append(jnp.max(earlier.astype(F32), axis=0, keepdims=True))
    load = gain_all * jnp.concatenate(load, 1)
    first = 1.0 - jnp.concatenate(first, 1)

    @pl.loop(0, nodes // LANES)
    def _(r):
        at = pl.ds(pl.multiple_of(r * LANES, LANES), LANES)
        pick[at, :] = (iota((LANES, nt), 0) + r * LANES == index).astype(F32).astype(BF16)

    wide = 2 * LANES

    @pl.loop(0, nt // wide)
    def _(c):
        at = pl.ds(pl.multiple_of(c * wide, wide), wide)
        for half in range(2):
            rows = slice(half * block, (half + 1) * block)
            picked[rows, at] = dot(inv2[rows, :], pick[:, at]).astype(BF16)

    index_col = column(index.astype(F32))
    for w in range(0, block, LANES):
        node = (iota((nt, LANES), 1) + (w + j * block)).astype(F32)
        own_pick[:, w : w + LANES] = (index_col == node).astype(F32).astype(BF16)
    mixed = dot3(same[...], own_pick[0:np_, :], ROWS)
    for w in range(0, block, LANES):
        at = slice(w, w + LANES)
        value = mixed[:, at] * gain_col
        high_ = value.astype(BF16)
        left[0:np_, at] = high_
        left[np_ : 2 * np_, at] = (value - high_.astype(F32)).astype(BF16)
    left[2 * np_ :, :] = own_pick[np_:, :]
    upper = dot(left[...], picked[0:block, :])
    lower = dot(left[0:np_, :], picked[block:, :])
    value = upper[0:np_] + (upper[np_ : 2 * np_] + lower)
    high_ = value.astype(BF16)
    mat[0:np_, 0:nt] = high_
    mat[0:np_, nt:] = (value - high_.astype(F32)).astype(BF16)
    mat[np_:, 0:nt] = upper[2 * np_ :].astype(BF16)
    mat[np_:, nt:] = dot(left[2 * np_ :, :], picked[block:, :]).astype(BF16)

    def tile_of(x, device):
        out = x[:, 0:LANES]
        for t in range(1, tiles):
            out = jnp.where(device // pack == t, x[:, t * LANES : (t + 1) * LANES], out)
        return out

    when(has_above, [gain_z], "wait_recv")
    when(has_right, [gain_x], "wait_recv")
    at_x = slice(cx - 1, cx)

    for n in range(STEPS):
        slab, up, down = y_copies(n)
        for copy in slab:
            copy.wait_recv()
        when(has_below, up, "wait_recv")
        when(has_above, down, "wait_recv")
        total, v_below, v_above = y[n, 0], below[n, 0], above[n, 0]
        for k in range(1, nj):
            total = total + y[n, k]
            v_below = v_below + below[n, k]
            v_above = v_above + above[n, k]
        v_near = jnp.concatenate([total[:, np_ : np_ + lines], v_below], 0)
        v_far = jnp.concatenate([v_above, total[:, np_ + lines :]], 0)
        waves_a.append(scale * v_near - in_a)
        waves_b.append(scale * v_far - in_b)
        change = total[:, 0:np_] - load * ez
        if n + 1 < STEPS:
            for copy in pre_copies(n + 1):
                copy.wait_recv()
            ez = change + pre[n + 1, 0]
            for k in range(1, nj):
                ez = ez + pre[n + 1, k]
            in_a, in_b, src = sources(n + 1, ez)
            x = fold3(src)
            send_y(n + 1, sum3(dot(jnp.concatenate([x, x], 1), mat[...], COLS)))
        change = change * first
        drop = dot3(cell_row[...] * tile_of(change, j), cell_y[...], COLS)

        when(has_below, [down_z(n)], "wait_send")

        @pl.when(has_left)
        def _():
            up_x(n).wait_recv()
            for z in range(cz):
                g = gain[z, 0:1, :]
                e[1, z, 0:1, :] = e[1, z, 0:1, :] + g * hx[n, 1, z : z + 1, :]
                e[2, z, 0:1, :] = e[2, z, 0:1, :] - g * hx[n, 0, z : z + 1, :]

        @pl.when(has_below)
        def _():
            up_z(n).wait_recv()
            g = gain[0]
            e[0, 0] = e[0, 0] + g * hz[n, 1]
            e[1, 0] = e[1, 0] - g * hz[n, 0]

        e[2] = e[2] + drop.reshape(cz, cx, ny)
        when(has_above & has_left, [corner_down(n)], "wait_recv")
        when(has_below & has_right, [corner_up(n)], "wait_recv")

        @pl.when(has_above)
        def _():
            down_z(n).wait_recv()
            e_top[0] = ez_up[n, 0] + gain_top[...] * h[1, cz - 1]
            e_top[1] = ez_up[n, 1] - gain_top[...] * h[0, cz - 1]
            e_top[1, 0:1, :] = e_top[1, 0:1, :] + gain_top[0:1, :] * corner_a[n]
            up_z(n).wait_send()

        drop_right = dot3(row_right[...] * tile_of(change, right_id), y_right[...], COLS)
        update_h()

        @pl.when(has_right)
        def _():
            down_x(n).wait_recv()
            g = gain_right[...]
            face_y = ex[n, 0] + g * hx_send[n, 1]
            face_z = ex[n, 1] - g * hx_send[n, 0] + drop_right
            for z in range(cz):
                y_ = face_y[z : z + 1]
                if z == 0:
                    y_ = y_ - g[0:1] * corner_b[n]
                h[1, z, at_x, :] = h[1, z, at_x, :] + 0.5 * face_z[z : z + 1]
                h[2, z, at_x, :] = h[2, z, at_x, :] - 0.5 * y_

        if n + 1 < STEPS:
            send_h(n + 1)
            update_e()
            if n + 2 < STEPS:
                send_pre(n + 2)
            send_e(n + 1)
        if n + 2 == STEPS:
            volt_out[...] = own_volts(src)

    wave_out[0, 0:1, :] = waves_a[-1][0:1]
    wave_out[0, 1:2, :] = waves_b[-1][0:1]

    for copy in info_copies:
        copy.wait_send()
    when(has_above, [line_copy], "wait_send")
    when(has_below, [gain_z], "wait_send")
    when(has_left, [gain_x], "wait_send")
    for n in range(STEPS):
        slab, up, down = y_copies(n)
        for copy in slab:
            copy.wait_send()
        when(has_above, up, "wait_send")
        when(has_below, down, "wait_send")
        if n:
            for copy in pre_copies(n):
                copy.wait_send()
        when(has_right, [up_x(n)], "wait_send")
        when(has_left, [down_x(n)], "wait_send")
        when(has_below & has_right, [corner_down(n)], "wait_send")
        when(has_above & has_left, [corner_up(n)], "wait_send")


def local(*args):
    e_field, inverse = args[0], args[7]
    nj = lax.axis_size("fxy")
    _, cz, cx, ny = e_field.shape
    _, block, nodes = inverse.shape
    ports, lines = args[4].shape[1], args[8].shape[1]
    args = [*args[:12], *(a.transpose(1, 0, 2) for a in args[12:])]
    depth = args[12].shape[0]
    vmem = pl.BlockSpec(memory_space=pltpu.VMEM)
    hbm = pl.BlockSpec(memory_space=pltpu.HBM)
    small = [a for i, a in enumerate(args) if i not in (0, 1, 2, 3, 7)]
    rows = -(-nj // 16) * 16
    np_ = nj * ports
    nt = np_ + 2 * lines
    line_rows = -(-(3 + 2 * depth) // 8) * 8
    dma = pltpu.SemaphoreType.DMA
    v = pltpu.VMEM
    return pl.pallas_call(
        kernel,
        out_shape=(
            v(e_field.shape, F32),
            v(e_field.shape, F32),
            v((1, block), F32),
            v((1, 2, lines), F32),
        ),
        in_specs=[hbm] * len(args),
        out_specs=(vmem,) * 4,
        scratch_shapes=[
            *[v(a.shape, a.dtype) for a in small],
            v((2, cx, ny), F32),
            v((cz, cx, ny), F32),
            v((cz, cx, ny), F32),
            v((cx, ny), F32),
            v((cz, ny), F32),
            v((cz, ny), F32),
            v((block, nodes), F32),
            v((2 * block, nodes), BF16),
            v((nodes, nt), BF16),
            v((2 * block, nt), BF16),
            v((nt, block), BF16),
            v((np_, np_), F32),
            v((2 * np_ + 2 * lines, block), BF16),
            v((nt, 2 * nt), BF16),
            v((cz * cx, LANES), F32),
            v((ny, LANES), BF16),
            v((cz, LANES), F32),
            v((ny, LANES), BF16),
            v((rows, nt), F32),
            v((block, nt), BF16),
            v((8, LANES), F32),
            v((8, LANES), F32),
            v((nj, 8, LANES), F32),
            v((line_rows, lines), F32),
            v((line_rows, lines), F32),
            v((STEPS, 1, np_), F32),
            v((STEPS, nj, 1, np_), F32),
            v((STEPS, 1, nt), F32),
            v((STEPS, nj, 1, nt), F32),
            v((STEPS, nj, 1, lines), F32),
            v((STEPS, nj, 1, lines), F32),
            v((STEPS, 2, cx, ny), F32),
            v((STEPS, 2, cx, ny), F32),
            v((STEPS, 2, cz, ny), F32),
            v((STEPS, 2, cz, ny), F32),
            v((STEPS, 2, cz, ny), F32),
            v((STEPS, 2, cz, ny), F32),
            v((STEPS, 2, 1, ny), F32),
            v((STEPS, 1, ny), F32),
            v((STEPS, 1, ny), F32),
            v((block, LANES), F32),
            dma((5 + len(small),)),
            dma((7, STEPS)),
            dma((7, STEPS)),
            dma((nj - 1,)),
            dma((nj - 1,)),
            dma((STEPS, nj - 1)),
            dma((STEPS, nj - 1)),
            dma((STEPS, nj - 1)),
            dma((STEPS, nj - 1)),
            dma((STEPS, nj)),
            dma((STEPS, nj)),
            dma((STEPS, nj)),
            dma((STEPS, nj)),
        ],
        compiler_params=pltpu.CompilerParams(
            collective_id=0, has_side_effects=True, vmem_limit_bytes=61 * 1024 * 1024
        ),
    )(*args)


def solution(mesh):
    placed = (
        P(None, "fz", "fxy", None),
        P(None, "fz", "fxy", None),
        P("fz", "fxy", None),
        P("fz", "fxy", None),
        P("fz", "fxy"),
        P("fz", "fxy"),
        P("fz", "fxy"),
        P("fz", "fxy", None),
        P("fz", None),
        P("fz", None),
        P("fz", None),
        P("fz", None),
        P("fz", None, None),
        P("fz", None, None),
    )
    return jax.shard_map(
        local,
        mesh=mesh,
        in_specs=placed,
        out_specs=(
            P(None, "fz", "fxy", None),
            P(None, "fz", "fxy", None),
            P("fz", "fxy"),
            P("fz", None, None),
        ),
        check_vma=False,
    )
```

time: 53.4 us -> 39.8 us (0.75)
  Pallas kernels: 45.9 us -> 35.9 us
  local copies, waits for them, and re-layouts: 6.64 us -> 2.9 us
    pallas_call x1, Pallas kernels: 45.9 us -> 35.9 us  [local(): pl.pallas_call(kernel, out_shape=(v(e_field.shape, F32), v(e_field.shape,...]
    unnamed x4, local copies, waits for them, and re-layouts: 6.64 us -> 2.9 us
where the time goes in v1:
time: 39.8 us; the launch traced here: 39.5 us
  Pallas kernels  35.9 us (90%)
  local copies, waits for them, and re-layouts  2.9 us (7%)
  between operations  0.65 us (2%)
    pallas_call x1, Pallas kernels, local(): pl.pallas_call(kernel, out_shape=(v(e_field.shape, F32), v(e_field.shape,...  35.9 us
    unnamed x4, local copies, waits for them, and re-layouts  2.9 us

profile of v1, /device:TPU:0, one launch (start us, length us, event | category | flops | bytes accessed | tf_op | source)
XLA Modules:
  0.0 39.5 jit_solution(2715060683592525560)
XLA Ops:
  0.6 35.9 %shard_map.165 = (f32[3,8,16,512]{3,2,1,0:T(8,128)S(1)}, f32[3,8,16,512]{3,2,1,0:T(8,128)S(1)}, f32[1,512]{1,0:T(1,128)S(1)}, f32[1,2,128]{2,1,0:T(2,128)S(1)}) custom-call(f32[3,8,16,512]{3,2,1,0:T(8,128)} %e_in.1, f32[3,8,16,512]{3,2,1,0:T(8,128)} %h_in.1, f32[8,16,512]{2,1,0:T(8,128)} %decay_in.1, f32[8,16,512]{2,1,0:T(8,128)} %gain_in.1, ...), custom_call_target="tpu_custom_call" | custom-call | tf_op jit(solution)/shard_map/pallas_call | solution.py:613
  36.6 0.9 %copy.22 = f32[3,8,16,512]{3,2,1,0:T(8,128)} copy(f32[3,8,16,512]{3,2,1,0:T(8,128)S(1)} %get-tuple-element.4) | data formatting | bytes 1572864
  37.5 0.6 %copy.25 = f32[1,2,128]{2,1,0:T(2,128)} copy(f32[1,2,128]{2,1,0:T(2,128)S(1)} %get-tuple-element.7) | data formatting | bytes 2048
  38.0 0.6 %copy.24 = f32[1,512]{1,0:T(1,128)} copy(f32[1,512]{1,0:T(1,128)S(1)} %get-tuple-element.6) | data formatting | bytes 4096
  38.6 0.9 %copy.23 = f32[3,8,16,512]{3,2,1,0:T(8,128)} copy(f32[3,8,16,512]{3,2,1,0:T(8,128)S(1)} %get-tuple-element.5) | data formatting | bytes 1572864

commit v2 on v1

--- a/solution.py
+++ b/solution.py
@@ -610,7 +610,7 @@
     line_rows = -(-(3 + 2 * depth) // 8) * 8
     dma = pltpu.SemaphoreType.DMA
     v = pltpu.VMEM
-    return pl.pallas_call(
+    e, h, volt, wave = pl.pallas_call(
         kernel,
         out_shape=(
             v(e_field.shape, F32),
@@ -681,6 +681,23 @@
             collective_id=0, has_side_effects=True, vmem_limit_bytes=61 * 1024 * 1024
         ),
     )(*args)
+    outs = [pltpu.with_memory_space_constraint(x, pltpu.VMEM) for x in (e, h, volt, wave)]
+    return pl.pallas_call(
+        store,
+        out_shape=[jax.ShapeDtypeStruct(x.shape, F32) for x in outs],
+        in_specs=[vmem] * 4,
+        out_specs=[hbm] * 4,
+        scratch_shapes=[dma((4,))],
+    )(*outs)
+
+
+def store(e, h, volt, wave, e_out, h_out, volt_out, wave_out, sem):
+    pairs = ((e, e_out), (h, h_out), (volt, volt_out), (wave, wave_out))
+    copies = [pltpu.make_async_copy(a, b, sem.at[k]) for k, (a, b) in enumerate(pairs)]
+    for copy in copies:
+        copy.start()
+    for copy in copies:
+        copy.wait()
 
 
 def solution(mesh):

time: 39.8 us -> 38.2 us (0.960)
  local copies, waits for them, and re-layouts: 2.9 us -> 0 us
  Pallas kernels: 35.9 us -> 37.2 us
    unnamed x4 -> x0, local copies, waits for them, and re-layouts: 2.9 us -> none
    pallas_call x0 -> x1, Pallas kernels: none -> 1.18 us  [local(): pl.pallas_call(store, out_shape=[jax.ShapeDtypeStruct(x.shape, F32) for x...]
where the time goes in v2:
time: 38.2 us; the launch traced here: 37.8 us
  Pallas kernels  37.2 us (97%)
  between operations  0.64 us (2%)
    pallas_call x1, Pallas kernels, local(): pl.pallas_call(kernel, out_shape=(v(e_field.shape, F32), v(e_field.shape,...  36 us
    pallas_call x1, Pallas kernels, local(): pl.pallas_call(store, out_shape=[jax.ShapeDtypeStruct(x.shape, F32) for x...  1.18 us

profile of v2, /device:TPU:0, one launch (start us, length us, event | category | flops | bytes accessed | tf_op | source)
XLA Modules:
  0.0 37.8 jit_solution(13399081204555475771)
XLA Ops:
  0.6 36.0 %shard_map.165 = (f32[3,8,16,512]{3,2,1,0:T(8,128)S(1)}, f32[3,8,16,512]{3,2,1,0:T(8,128)S(1)}, f32[1,512]{1,0:T(1,128)S(1)}, f32[1,2,128]{2,1,0:T(2,128)S(1)}) custom-call(f32[3,8,16,512]{3,2,1,0:T(8,128)} %e_in.1, f32[3,8,16,512]{3,2,1,0:T(8,128)} %h_in.1, f32[8,16,512]{2,1,0:T(8,128)} %decay_in.1, f32[8,16,512]{2,1,0:T(8,128)} %gain_in.1, ...), custom_call_target="tpu_custom_call" | custom-call | tf_op jit(solution)/shard_map/pallas_call | solution.py:613
  36.7 1.2 %shard_map.166 = (f32[3,8,16,512]{3,2,1,0:T(8,128)}, f32[3,8,16,512]{3,2,1,0:T(8,128)}, f32[1,512]{1,0:T(1,128)}, f32[1,2,128]{2,1,0:T(2,128)}) custom-call(f32[3,8,16,512]{3,2,1,0:T(8,128)S(1)} %get-tuple-element.8.e, f32[3,8,16,512]{3,2,1,0:T(8,128)S(1)} %get-tuple-element.9.h, f32[1,512]{1,0:T(1,128)S(1)} %get-tuple-element.10.volt, ...), custom_call_target="tpu_custom_call" | custom-call | tf_op jit(solution)/shard_map/pallas_call | solution.py:685

commit v3 on v2

--- a/solution.py
+++ b/solution.py
@@ -246,7 +246,7 @@
 
         plane(0, None)
 
-        @pl.loop(1, cz)
+        @pl.loop(1, cz, unroll=True)
         def _(z):
             plane(z, z - 1)
 
@@ -264,7 +264,7 @@
             h[1, z] = h[1, z] - 0.5 * ((ux - ex_) - dx(ez_))
             h[2, z] = h[2, z] - 0.5 * (dx(ey_) - dy(ex_))
 
-        @pl.loop(0, cz - 1)
+        @pl.loop(0, cz - 1, unroll=True)
         def _(z):
             plane(z, e[0, z + 1], e[1, z + 1])
 

time: 38.2 us -> 34.9 us (0.914)
  Pallas kernels: 37.2 us -> 34.1 us
    pallas_call x1, Pallas kernels: 36 us -> 32.9 us  [local(): pl.pallas_call(kernel, out_shape=(v(e_field.shape, F32), v(e_field.shape,...]
where the time goes in v3:
time: 34.9 us; the launch traced here: 34.7 us
  Pallas kernels  34.1 us (98%)
  between operations  0.64 us (2%)
    pallas_call x1, Pallas kernels, local(): pl.pallas_call(kernel, out_shape=(v(e_field.shape, F32), v(e_field.shape,...  32.9 us
    pallas_call x1, Pallas kernels, local(): pl.pallas_call(store, out_shape=[jax.ShapeDtypeStruct(x.shape, F32) for x...  1.18 us

profile of v3, /device:TPU:0, one launch (start us, length us, event | category | flops | bytes accessed | tf_op | source)
XLA Modules:
  0.0 34.7 jit_solution(15922411310460975617)
XLA Ops:
  0.6 32.9 %shard_map.165 = (f32[3,8,16,512]{3,2,1,0:T(8,128)S(1)}, f32[3,8,16,512]{3,2,1,0:T(8,128)S(1)}, f32[1,512]{1,0:T(1,128)S(1)}, f32[1,2,128]{2,1,0:T(2,128)S(1)}) custom-call(f32[3,8,16,512]{3,2,1,0:T(8,128)} %e_in.1, f32[3,8,16,512]{3,2,1,0:T(8,128)} %h_in.1, f32[8,16,512]{2,1,0:T(8,128)} %decay_in.1, f32[8,16,512]{2,1,0:T(8,128)} %gain_in.1, ...), custom_call_target="tpu_custom_call" | custom-call | tf_op jit(solution)/shard_map/pallas_call | solution.py:613
  33.6 1.2 %shard_map.166 = (f32[3,8,16,512]{3,2,1,0:T(8,128)}, f32[3,8,16,512]{3,2,1,0:T(8,128)}, f32[1,512]{1,0:T(1,128)}, f32[1,2,128]{2,1,0:T(2,128)}) custom-call(f32[3,8,16,512]{3,2,1,0:T(8,128)S(1)} %get-tuple-element.8.e, f32[3,8,16,512]{3,2,1,0:T(8,128)S(1)} %get-tuple-element.9.h, f32[1,512]{1,0:T(1,128)S(1)} %get-tuple-element.10.volt, ...), custom_call_target="tpu_custom_call" | custom-call | tf_op jit(solution)/shard_map/pallas_call | solution.py:685

commit v4 on v3

--- a/solution.py
+++ b/solution.py
@@ -107,7 +107,7 @@
         pltpu.make_async_copy(src, dst, load_sem.at[5 + k])
         for k, (src, dst) in enumerate(small)
     ]
-    for copy in small + loads:
+    for copy in small + loads[:4]:
         copy.start()
 
     e_top[...] = jnp.zeros(e_top.shape, F32)
@@ -119,11 +119,7 @@
 
     barrier = pltpu.get_barrier_semaphore()
     for other in (above_id, below_id):
-        for d in range(nj):
-            pl.semaphore_signal(
-                barrier, inc=1, device_id={"fz": other, "fxy": lax.rem(j + d, nj)},
-                device_id_type=MESH,
-            )
+        pl.semaphore_signal(barrier, inc=1, device_id={"fz": other}, device_id_type=MESH)
     for d in range(1, nj):
         pl.semaphore_signal(
             barrier, inc=1, device_id={"fxy": lax.rem(j + d, nj)}, device_id_type=MESH
@@ -205,14 +201,18 @@
         for copy in slab:
             copy.start()
 
-    def send_h(n):
+    def pack_h(n):
         for c in range(2):
             for z in range(cz):
                 hx_send[n, c, z : z + 1, :] = h[1 + c, z, cx - 1 : cx, :]
         corner_send[n, 0] = h[2, 0, cx - 1 : cx, :]
         corner_send[n, 1] = h[0, cz - 1, 0:1, :]
+
+    def send_h(n):
         when(has_above, [up_z(n)], "start")
         when(has_right, [up_x(n)], "start")
+
+    def send_corners(n):
         when(has_below & has_right, [corner_down(n)], "start")
         when(has_above & has_left, [corner_up(n)], "start")
 
@@ -226,29 +226,24 @@
     lane = iota((cx, ny), 1)
     sub = iota((cx, ny), 0)
 
-    def update_e():
-        def plane(z, lower):
-            hx_, hy_, hz_ = (h[c, z] for c in range(3))
-            dx, dy = hx_, hy_
-            if lower is not None:
-                dx, dy = hx_ - h[0, lower], hy_ - h[1, lower]
-
-            def by(f):
-                return f - jnp.where(lane == 0, 0.0, pltpu.roll(f, 1, 1))
-
-            def bx(f):
-                return f - jnp.where(sub == 0, 0.0, pltpu.roll(f, 1, 0))
-
-            g, q = gain[z], decay[z]
-            e[0, z] = q * e[0, z] + g * (by(hz_) - dy)
-            e[1, z] = q * e[1, z] + g * (dx - bx(hz_))
-            e[2, z] = q * e[2, z] + g * (bx(hy_) - by(hx_))
-
-        plane(0, None)
-
-        @pl.loop(1, cz, unroll=True)
-        def _(z):
-            plane(z, z - 1)
+    def by(f):
+        return f - jnp.where(lane == 0, 0.0, pltpu.roll(f, 1, 1))
+
+    def bx(f):
+        return f - jnp.where(sub == 0, 0.0, pltpu.roll(f, 1, 0))
+
+
+    def update_ez():
+        for z in range(cz):
+            e[2, z] = decay[z] * e[2, z] + gain[z] * (bx(h[1, z]) - by(h[0, z]))
+
+    def update_exy():
+        for z in range(cz):
+            dx, dy, hz_ = h[0, z], h[1, z], h[2, z]
+            if z:
+                dx, dy = dx - h[0, z - 1], dy - h[1, z - 1]
+            e[0, z] = decay[z] * e[0, z] + gain[z] * (by(hz_) - dy)
+            e[1, z] = decay[z] * e[1, z] + gain[z] * (dx - bx(hz_))
 
     def update_h():
         def plane(z, ux, uy):
@@ -300,6 +295,7 @@
         return jnp.sum(value * cell_row[...], axis=0, keepdims=True)
 
     loads[0].wait()
+    loads[4].start()
     info_send[4:5, :] = gather_cells(e[2])
     loads[1].wait()
     info_send[3:4, :] = gather_cells(gain[...])
@@ -307,17 +303,19 @@
         gain_send[z : z + 1, :] = gain[z, 0:1, :]
     info[j] = info_send[...]
 
-    pl.semaphore_wait(barrier, nj - 1 + 2 * nj)
+    pl.semaphore_wait(barrier, nj + 1)
     for copy in info_copies:
         copy.start()
     when(has_above, [line_copy], "start")
+    when(has_below, [gain_z], "start")
     loads[2].wait()
+    pack_h(0)
     send_h(0)
+    when(has_left, [gain_x], "start")
     loads[3].wait()
-    update_e()
+    update_ez()
+    update_exy()
     send_e(0)
-    when(has_below, [gain_z], "start")
-    when(has_left, [gain_x], "start")
     loads[4].wait()
 
     chunk = 32
@@ -332,7 +330,26 @@
             x - high.astype(F32)
         ).astype(BF16)
 
+    wide = 2 * LANES
+
+    def take_columns(first, last, index):
+        @pl.loop(0, nodes // LANES)
+        def _(r):
+            at = pl.ds(pl.multiple_of(r * LANES, LANES), LANES)
+            hit = iota((LANES, last - first), 0) + r * LANES == index
+            pick[at, first:last] = hit.astype(F32).astype(BF16)
+
+        for c in range(first, last, wide):
+            at = slice(c, min(c + wide, last))
+            for half in range(2):
+                rows = slice(half * block, (half + 1) * block)
+                picked[rows, at] = dot(inv2[rows, :], pick[:, at]).astype(BF16)
+
+    when(has_above, [gain_z], "wait_recv")
     when(has_below, [line_copy], "wait_recv")
+    send_corners(0)
+    near_far = jnp.concatenate([line_near[...], line_info[0:1, :].astype(I32) - 1], 1)
+    take_columns(np_, nt, near_far)
     for copy in info_copies:
         copy.wait_recv()
 
@@ -341,8 +358,7 @@
     )
     cell_all = everyone[0:1] - 1.0
     cond_all, gain_all = everyone[2:3], everyone[3:4]
-    near_far = [line_near[...], line_info[0:1, :].astype(I32) - 1]
-    index = jnp.concatenate([everyone[1:2].astype(I32) - 1, *near_far], 1)
+    index = jnp.concatenate([everyone[1:2].astype(I32) - 1, near_far], 1)
     high = jnp.where(index >= 0, index // block, -1)
     low = jnp.where(index >= 0, index % block, -1)
     node_hi[...] = (iota(node_hi.shape, 0) == high).astype(F32)
@@ -443,20 +459,7 @@
     load = gain_all * jnp.concatenate(load, 1)
     first = 1.0 - jnp.concatenate(first, 1)
 
-    @pl.loop(0, nodes // LANES)
-    def _(r):
-        at = pl.ds(pl.multiple_of(r * LANES, LANES), LANES)
-        pick[at, :] = (iota((LANES, nt), 0) + r * LANES == index).astype(F32).astype(BF16)
-
-    wide = 2 * LANES
-
-    @pl.loop(0, nt // wide)
-    def _(c):
-        at = pl.ds(pl.multiple_of(c * wide, wide), wide)
-        for half in range(2):
-            rows = slice(half * block, (half + 1) * block)
-            picked[rows, at] = dot(inv2[rows, :], pick[:, at]).astype(BF16)
-
+    take_columns(0, np_, index[:, 0:np_])
     index_col = column(index.astype(F32))
     for w in range(0, block, LANES):
         node = (iota((nt, LANES), 1) + (w + j * block)).astype(F32)
@@ -484,7 +487,6 @@
             out = jnp.where(device // pack == t, x[:, t * LANES : (t + 1) * LANES], out)
         return out
 
-    when(has_above, [gain_z], "wait_recv")
     when(has_right, [gain_x], "wait_recv")
     at_x = slice(cx - 1, cx)
 
@@ -504,6 +506,27 @@
         waves_a.append(scale * v_near - in_a)
         waves_b.append(scale * v_far - in_b)
         change = total[:, 0:np_] - load * ez
+        once = change * first
+        drop = dot3(cell_row[...] * tile_of(once, j), cell_y[...], COLS)
+
+        when(has_below, [down_z(n)], "wait_send")
+
+        @pl.when(has_left)
+        def _():
+            up_x(n).wait_recv()
+            for z in range(cz):
+                g = gain[z, 0:1, :]
+                e[1, z, 0:1, :] = e[1, z, 0:1, :] + g * hx[n, 1, z : z + 1, :]
+                e[2, z, 0:1, :] = e[2, z, 0:1, :] - g * hx[n, 0, z : z + 1, :]
+
+        @pl.when(has_below)
+        def _():
+            up_z(n).wait_recv()
+            g = gain[0]
+            e[0, 0] = e[0, 0] + g * hz[n, 1]
+            e[1, 0] = e[1, 0] - g * hz[n, 0]
+
+        e[2] = e[2] + drop.reshape(cz, cx, ny)
         if n + 1 < STEPS:
             for copy in pre_copies(n + 1):
                 copy.wait_recv()
@@ -513,27 +536,6 @@
             in_a, in_b, src = sources(n + 1, ez)
             x = fold3(src)
             send_y(n + 1, sum3(dot(jnp.concatenate([x, x], 1), mat[...], COLS)))
-        change = change * first
-        drop = dot3(cell_row[...] * tile_of(change, j), cell_y[...], COLS)
-
-        when(has_below, [down_z(n)], "wait_send")
-
-        @pl.when(has_left)
-        def _():
-            up_x(n).wait_recv()
-            for z in range(cz):
-                g = gain[z, 0:1, :]
-                e[1, z, 0:1, :] = e[1, z, 0:1, :] + g * hx[n, 1, z : z + 1, :]
-                e[2, z, 0:1, :] = e[2, z, 0:1, :] - g * hx[n, 0, z : z + 1, :]
-
-        @pl.when(has_below)
-        def _():
-            up_z(n).wait_recv()
-            g = gain[0]
-            e[0, 0] = e[0, 0] + g * hz[n, 1]
-            e[1, 0] = e[1, 0] - g * hz[n, 0]
-
-        e[2] = e[2] + drop.reshape(cz, cx, ny)
         when(has_above & has_left, [corner_down(n)], "wait_recv")
         when(has_below & has_right, [corner_up(n)], "wait_recv")
 
@@ -545,7 +547,7 @@
             e_top[1, 0:1, :] = e_top[1, 0:1, :] + gain_top[0:1, :] * corner_a[n]
             up_z(n).wait_send()
 
-        drop_right = dot3(row_right[...] * tile_of(change, right_id), y_right[...], COLS)
+        drop_right = dot3(row_right[...] * tile_of(once, right_id), y_right[...], COLS)
         update_h()
 
         @pl.when(has_right)
@@ -562,10 +564,13 @@
                 h[2, z, at_x, :] = h[2, z, at_x, :] - 0.5 * y_
 
         if n + 1 < STEPS:
-            send_h(n + 1)
-            update_e()
+            pack_h(n + 1)
+            update_ez()
             if n + 2 < STEPS:
                 send_pre(n + 2)
+            send_h(n + 1)
+            send_corners(n + 1)
+            update_exy()
             send_e(n + 1)
         if n + 2 == STEPS:
             volt_out[...] = own_volts(src)

time: 34.9 us -> 33.6 us (0.963)
  the two profiles are of different devices: /device:TPU:0 before, /device:TPU:1 now
where the time goes in v4:
time: 33.6 us; the launch traced here: 33.5 us
  Pallas kernels  32.8 us (98%)
  between operations  0.64 us (2%)
    pallas_call x1, Pallas kernels, local(): pl.pallas_call(kernel, out_shape=(v(e_field.shape, F32), v(e_field.shape,...  31.6 us
    pallas_call x1, Pallas kernels, local(): pl.pallas_call(store, out_shape=[jax.ShapeDtypeStruct(x.shape, F32) for x...  1.18 us

profile of v4, /device:TPU:1, one launch (start us, length us, event | category | flops | bytes accessed | tf_op | source)
XLA Modules:
  0.0 33.5 jit_solution(13192526429332896084)
XLA Ops:
  0.6 31.6 %shard_map.165 = (f32[3,8,16,512]{3,2,1,0:T(8,128)S(1)}, f32[3,8,16,512]{3,2,1,0:T(8,128)S(1)}, f32[1,512]{1,0:T(1,128)S(1)}, f32[1,2,128]{2,1,0:T(2,128)S(1)}) custom-call(f32[3,8,16,512]{3,2,1,0:T(8,128)} %e_in.1, f32[3,8,16,512]{3,2,1,0:T(8,128)} %h_in.1, f32[8,16,512]{2,1,0:T(8,128)} %decay_in.1, f32[8,16,512]{2,1,0:T(8,128)} %gain_in.1, ...), custom_call_target="tpu_custom_call" | custom-call | tf_op jit(solution)/shard_map/pallas_call | solution.py:618
  32.3 1.2 %shard_map.166 = (f32[3,8,16,512]{3,2,1,0:T(8,128)}, f32[3,8,16,512]{3,2,1,0:T(8,128)}, f32[1,512]{1,0:T(1,128)}, f32[1,2,128]{2,1,0:T(2,128)}) custom-call(f32[3,8,16,512]{3,2,1,0:T(8,128)S(1)} %get-tuple-element.8.e, f32[3,8,16,512]{3,2,1,0:T(8,128)S(1)} %get-tuple-element.9.h, f32[1,512]{1,0:T(1,128)S(1)} %get-tuple-element.10.volt, ...), custom_call_target="tpu_custom_call" | custom-call | tf_op jit(solution)/shard_map/pallas_call | solution.py:690

commit v5 on v4

--- a/solution.py
+++ b/solution.py
@@ -67,7 +67,7 @@
     e, h, volt_out, wave_out,
     port_cell, port_node, port_cond, line_near, line_far, line_delay, line_imped,
     hist_near, hist_far,
-    e_top, decay, gain, gain_top, gain_send, gain_right, inv, inv2, pick, picked, own_pick,
+    decay, gain, gain_top, gain_send, gain_right, inv, inv2, pick, picked, own_pick,
     same, left, mat, cell_row, cell_y, row_right, y_right, node_hi, node_lo, pads,
     info_send, info, line_send, line_info, pre_send, pre, y_send, y, below, above,
     hz, ez_up, hx_send, hx, ex_send, ex, corner_send, corner_a, corner_b, acc,
@@ -110,7 +110,6 @@
     for copy in small + loads[:4]:
         copy.start()
 
-    e_top[...] = jnp.zeros(e_top.shape, F32)
     below[...] = jnp.zeros(below.shape, F32)
     above[...] = jnp.zeros(above.shape, F32)
     corner_a[...] = jnp.zeros(corner_a.shape, F32)
@@ -124,6 +123,18 @@
         pl.semaphore_signal(
             barrier, inc=1, device_id={"fxy": lax.rem(j + d, nj)}, device_id_type=MESH
         )
+
+    for missing, refs in (
+        (jnp.logical_not(has_below), (hz,)),
+        (jnp.logical_not(has_above), (ez_up, gain_top)),
+        (jnp.logical_not(has_left), (hx,)),
+        (jnp.logical_not(has_right), (ex, gain_right)),
+    ):
+
+        @pl.when(missing)
+        def _(refs=refs):
+            for ref in refs:
+                ref[...] = jnp.zeros(ref.shape, F32)
 
     def remote(src, dst, ss, rs, **where):
         return pltpu.make_async_remote_copy(
@@ -245,7 +256,7 @@
             e[0, z] = decay[z] * e[0, z] + gain[z] * (by(hz_) - dy)
             e[1, z] = decay[z] * e[1, z] + gain[z] * (dx - bx(hz_))
 
-    def update_h():
+    def update_h(top):
         def plane(z, ux, uy):
             ex_, ey_, ez_ = (e[c, z] for c in range(3))
 
@@ -263,7 +274,7 @@
         def _(z):
             plane(z, e[0, z + 1], e[1, z + 1])
 
-        plane(cz - 1, e_top[0], e_top[1])
+        plane(cz - 1, *top)
 
     for copy in small:
         copy.wait()
@@ -349,7 +360,6 @@
     when(has_below, [line_copy], "wait_recv")
     send_corners(0)
     near_far = jnp.concatenate([line_near[...], line_info[0:1, :].astype(I32) - 1], 1)
-    take_columns(np_, nt, near_far)
     for copy in info_copies:
         copy.wait_recv()
 
@@ -390,7 +400,7 @@
     def own_volts(src):
         totals = dot3(node_hi[...] * src, node_lo[...], COLS)[0:nj]
 
-        @pl.loop(0, block // chunk)
+        @pl.loop(0, block // chunk, unroll=4)
         def _(r):
             at = pl.ds(pl.multiple_of(r * chunk, chunk), chunk)
             value = jnp.zeros((chunk, LANES), F32)
@@ -460,6 +470,7 @@
     first = 1.0 - jnp.concatenate(first, 1)
 
     take_columns(0, np_, index[:, 0:np_])
+    take_columns(np_, nt, index[:, np_:nt])
     index_col = column(index.astype(F32))
     for w in range(0, block, LANES):
         node = (iota((nt, LANES), 1) + (w + j * block)).astype(F32)
@@ -509,24 +520,6 @@
         once = change * first
         drop = dot3(cell_row[...] * tile_of(once, j), cell_y[...], COLS)
 
-        when(has_below, [down_z(n)], "wait_send")
-
-        @pl.when(has_left)
-        def _():
-            up_x(n).wait_recv()
-            for z in range(cz):
-                g = gain[z, 0:1, :]
-                e[1, z, 0:1, :] = e[1, z, 0:1, :] + g * hx[n, 1, z : z + 1, :]
-                e[2, z, 0:1, :] = e[2, z, 0:1, :] - g * hx[n, 0, z : z + 1, :]
-
-        @pl.when(has_below)
-        def _():
-            up_z(n).wait_recv()
-            g = gain[0]
-            e[0, 0] = e[0, 0] + g * hz[n, 1]
-            e[1, 0] = e[1, 0] - g * hz[n, 0]
-
-        e[2] = e[2] + drop.reshape(cz, cx, ny)
         if n + 1 < STEPS:
             for copy in pre_copies(n + 1):
                 copy.wait_recv()
@@ -536,32 +529,35 @@
             in_a, in_b, src = sources(n + 1, ez)
             x = fold3(src)
             send_y(n + 1, sum3(dot(jnp.concatenate([x, x], 1), mat[...], COLS)))
+        when(has_below, [down_z(n)], "wait_send")
+        when(has_above, [up_z(n)], "wait_send")
+        when(has_left, [up_x(n)], "wait_recv")
+        when(has_below, [up_z(n)], "wait_recv")
+        when(has_above, [down_z(n)], "wait_recv")
+        when(has_right, [down_x(n)], "wait_recv")
         when(has_above & has_left, [corner_down(n)], "wait_recv")
         when(has_below & has_right, [corner_up(n)], "wait_recv")
-
-        @pl.when(has_above)
-        def _():
-            down_z(n).wait_recv()
-            e_top[0] = ez_up[n, 0] + gain_top[...] * h[1, cz - 1]
-            e_top[1] = ez_up[n, 1] - gain_top[...] * h[0, cz - 1]
-            e_top[1, 0:1, :] = e_top[1, 0:1, :] + gain_top[0:1, :] * corner_a[n]
-            up_z(n).wait_send()
-
+        for z in range(cz):
+            g = gain[z, 0:1, :]
+            e[1, z, 0:1, :] = e[1, z, 0:1, :] + g * hx[n, 1, z : z + 1, :]
+            e[2, z, 0:1, :] = e[2, z, 0:1, :] - g * hx[n, 0, z : z + 1, :]
+        e[0, 0] = e[0, 0] + gain[0] * hz[n, 1]
+        e[1, 0] = e[1, 0] - gain[0] * hz[n, 0]
+        e[2] = e[2] + drop.reshape(cz, cx, ny)
+        top_x = ez_up[n, 0] + gain_top[...] * h[1, cz - 1]
+        side = jnp.where(sub == 0, gain_top[0:1, :] * corner_a[n], 0.0)
+        top_y = ez_up[n, 1] - gain_top[...] * h[0, cz - 1] + side
         drop_right = dot3(row_right[...] * tile_of(once, right_id), y_right[...], COLS)
-        update_h()
-
-        @pl.when(has_right)
-        def _():
-            down_x(n).wait_recv()
-            g = gain_right[...]
-            face_y = ex[n, 0] + g * hx_send[n, 1]
-            face_z = ex[n, 1] - g * hx_send[n, 0] + drop_right
-            for z in range(cz):
-                y_ = face_y[z : z + 1]
-                if z == 0:
-                    y_ = y_ - g[0:1] * corner_b[n]
-                h[1, z, at_x, :] = h[1, z, at_x, :] + 0.5 * face_z[z : z + 1]
-                h[2, z, at_x, :] = h[2, z, at_x, :] - 0.5 * y_
+        g = gain_right[...]
+        face_y = ex[n, 0] + g * hx_send[n, 1]
+        face_z = ex[n, 1] - g * hx_send[n, 0] + drop_right
+        update_h((top_x, top_y))
+        for z in range(cz):
+            y_ = face_y[z : z + 1]
+            if z == 0:
+                y_ = y_ - g[0:1] * corner_b[n]
+            h[1, z, at_x, :] = h[1, z, at_x, :] + 0.5 * face_z[z : z + 1]
+            h[2, z, at_x, :] = h[2, z, at_x, :] - 0.5 * y_
 
         if n + 1 < STEPS:
             pack_h(n + 1)
@@ -627,7 +623,6 @@
         out_specs=(vmem,) * 4,
         scratch_shapes=[
             *[v(a.shape, a.dtype) for a in small],
-            v((2, cx, ny), F32),
             v((cz, cx, ny), F32),
             v((cz, cx, ny), F32),
             v((cx, ny), F32),

time: 33.6 us -> 33.1 us (0.985)
  the two profiles are of different devices: /device:TPU:1 before, /device:TPU:0 now
where the time goes in v5:
time: 33.1 us; the launch traced here: 32.6 us
  Pallas kernels  32 us (97%)
  between operations  0.64 us (2%)
    pallas_call x1, Pallas kernels, local(): pl.pallas_call(kernel, out_shape=(v(e_field.shape, F32), v(e_field.shape,...  30.8 us
    pallas_call x1, Pallas kernels, local(): pl.pallas_call(store, out_shape=[jax.ShapeDtypeStruct(x.shape, F32) for x...  1.18 us

profile of v5, /device:TPU:0, one launch (start us, length us, event | category | flops | bytes accessed | tf_op | source)
XLA Modules:
  0.0 32.6 jit_solution(2995115984029405787)
XLA Ops:
  0.6 30.8 %shard_map.165 = (f32[3,8,16,512]{3,2,1,0:T(8,128)S(1)}, f32[3,8,16,512]{3,2,1,0:T(8,128)S(1)}, f32[1,512]{1,0:T(1,128)S(1)}, f32[1,2,128]{2,1,0:T(2,128)S(1)}) custom-call(f32[3,8,16,512]{3,2,1,0:T(8,128)} %e_in.1, f32[3,8,16,512]{3,2,1,0:T(8,128)} %h_in.1, f32[8,16,512]{2,1,0:T(8,128)} %decay_in.1, f32[8,16,512]{2,1,0:T(8,128)} %gain_in.1, ...), custom_call_target="tpu_custom_call" | custom-call | tf_op jit(solution)/shard_map/pallas_call | solution.py:614
  31.5 1.2 %shard_map.166 = (f32[3,8,16,512]{3,2,1,0:T(8,128)}, f32[3,8,16,512]{3,2,1,0:T(8,128)}, f32[1,512]{1,0:T(1,128)}, f32[1,2,128]{2,1,0:T(2,128)}) custom-call(f32[3,8,16,512]{3,2,1,0:T(8,128)S(1)} %get-tuple-element.8.e, f32[3,8,16,512]{3,2,1,0:T(8,128)S(1)} %get-tuple-element.9.h, f32[1,512]{1,0:T(1,128)S(1)} %get-tuple-element.10.volt, ...), custom_call_target="tpu_custom_call" | custom-call | tf_op jit(solution)/shard_map/pallas_call | solution.py:685

commit v6 on v5

--- a/solution.py
+++ b/solution.py
@@ -182,7 +182,7 @@
     def spread_z(src, dst, ss, rs, to):
         return [
             remote(src, dst, ss.at[d], rs.at[d], fz=to, fxy=lax.rem(j + d, nj))
-            for d in range(nj)
+            for d in (*range(1, nj), 0)
         ]
 
     info_copies = spread(info_send, info.at[j], info_ss, info_rs)
@@ -331,7 +331,7 @@
 
     chunk = 32
 
-    @pl.loop(0, block // chunk)
+    @pl.loop(0, block // chunk, unroll=4)
     def _(r):
         at = pl.ds(pl.multiple_of(r * chunk, chunk), chunk)
         x = inv[at, :]
@@ -344,7 +344,7 @@
     wide = 2 * LANES
 
     def take_columns(first, last, index):
-        @pl.loop(0, nodes // LANES)
+        @pl.loop(0, nodes // LANES, unroll=4)
         def _(r):
             at = pl.ds(pl.multiple_of(r * LANES, LANES), LANES)
             hit = iota((LANES, last - first), 0) + r * LANES == index
@@ -469,8 +469,7 @@
     load = gain_all * jnp.concatenate(load, 1)
     first = 1.0 - jnp.concatenate(first, 1)
 
-    take_columns(0, np_, index[:, 0:np_])
-    take_columns(np_, nt, index[:, np_:nt])
+    take_columns(0, nt, index)
     index_col = column(index.astype(F32))
     for w in range(0, block, LANES):
         node = (iota((nt, LANES), 1) + (w + j * block)).astype(F32)

time: 33.1 us -> 32.9 us (level)
  no operation moved by 1% of the time
where the time goes in v6:
time: 32.9 us; the launch traced here: 32.4 us
  Pallas kernels  31.8 us (97%)
  between operations  0.64 us (2%)
    pallas_call x1, Pallas kernels, local(): pl.pallas_call(kernel, out_shape=(v(e_field.shape, F32), v(e_field.shape,...  30.6 us
    pallas_call x1, Pallas kernels, local(): pl.pallas_call(store, out_shape=[jax.ShapeDtypeStruct(x.shape, F32) for x...  1.18 us

profile of v6, /device:TPU:0, one launch (start us, length us, event | category | flops | bytes accessed | tf_op | source)
XLA Modules:
  0.0 32.4 jit_solution(1108540878291447317)
XLA Ops:
  0.6 30.6 %shard_map.165 = (f32[3,8,16,512]{3,2,1,0:T(8,128)S(1)}, f32[3,8,16,512]{3,2,1,0:T(8,128)S(1)}, f32[1,512]{1,0:T(1,128)S(1)}, f32[1,2,128]{2,1,0:T(2,128)S(1)}) custom-call(f32[3,8,16,512]{3,2,1,0:T(8,128)} %e_in.1, f32[3,8,16,512]{3,2,1,0:T(8,128)} %h_in.1, f32[8,16,512]{2,1,0:T(8,128)} %decay_in.1, f32[8,16,512]{2,1,0:T(8,128)} %gain_in.1, ...), custom_call_target="tpu_custom_call" | custom-call | tf_op jit(solution)/shard_map/pallas_call | solution.py:613
  31.2 1.2 %shard_map.166 = (f32[3,8,16,512]{3,2,1,0:T(8,128)}, f32[3,8,16,512]{3,2,1,0:T(8,128)}, f32[1,512]{1,0:T(1,128)}, f32[1,2,128]{2,1,0:T(2,128)}) custom-call(f32[3,8,16,512]{3,2,1,0:T(8,128)S(1)} %get-tuple-element.8.e, f32[3,8,16,512]{3,2,1,0:T(8,128)S(1)} %get-tuple-element.9.h, f32[1,512]{1,0:T(1,128)S(1)} %get-tuple-element.10.volt, ...), custom_call_target="tpu_custom_call" | custom-call | tf_op jit(solution)/shard_map/pallas_call | solution.py:684
